TPU v7x, 8 devices: a whole 2x2x1 slice. The times are simulated.
8 devices in a mesh: dp: 1 (over z), ep: 8 (over y, x, core).
Axes of the slice: x: 2, y: 2, z: 1, core: 2. Of those that a mesh axis runs over, the one named last changes fastest.
Arguments:
- hidden: bfloat16 [768, 2048], P(('dp', 'ep'))
- norm_gain: bfloat16 [2048], replicated
- w_gate: bfloat16 [2048, 64], replicated
- w1_shared: bfloat16 [2048, 2816], replicated
- w3_shared: bfloat16 [2048, 2816], replicated
- w2_shared: bfloat16 [2816, 2048], replicated
- w1_experts: bfloat16 [64, 2048, 1408], P('ep')
- w3_experts: bfloat16 [64, 2048, 1408], P('ep')
- w2_experts: bfloat16 [64, 1408, 2048], P('ep')
- topk_ids: int32 [768, 6], P(('dp', 'ep'))
Outputs:
- output: bfloat16 [768, 2048], P(('dp', 'ep'))
All inputs are finite; a program needn't handle non-finite values.
Results may differ from a plain program's by a relative error of at most 0.00589404.
Values are sent between devices in bfloat16 or wider.
A program may use at most 1 GiB of HBM per device.

v0:
```python
import jax
import jax.numpy as jnp
from jax import lax
from jax.sharding import PartitionSpec as P

ROUTE_SCALE = 16
NORM_EPS = 1e-6


def rms_norm(hidden, norm_gain):
    rows_f = hidden.astype(jnp.float32)
    inv_rms = lax.rsqrt(jnp.mean(rows_f * rows_f, axis=-1, keepdims=True) + NORM_EPS)
    return (rows_f * inv_rms * norm_gain.astype(jnp.float32)).astype(jnp.bfloat16)


def swiglu(rows_in, w_up, w_lin, w_down):
    gate_act = jnp.dot(rows_in, w_up, preferred_element_type=jnp.float32)
    lin_act = jnp.dot(rows_in, w_lin, preferred_element_type=jnp.float32)
    inner_act = (jax.nn.silu(gate_act) * lin_act).astype(jnp.bfloat16)
    return jnp.dot(inner_act, w_down, preferred_element_type=jnp.float32).astype(jnp.bfloat16)


def router_weights(normed, w_gate, topk_ids):
    gate_probs = jax.nn.softmax(jnp.dot(normed, w_gate, preferred_element_type=jnp.float32), axis=-1)
    return ROUTE_SCALE * jnp.take_along_axis(gate_probs, topk_ids, axis=1)


def routed_experts(rows_in, row_wts, w1_experts, w3_experts, w2_experts):
    gate_act = jnp.einsum('nd,edf->enf', rows_in, w1_experts, preferred_element_type=jnp.float32)
    lin_act = jnp.einsum('nd,edf->enf', rows_in, w3_experts, preferred_element_type=jnp.float32)
    inner_act = (jax.nn.silu(gate_act) * lin_act).astype(jnp.bfloat16)
    expert_out = jnp.einsum('enf,efd->end', inner_act, w2_experts, preferred_element_type=jnp.float32).astype(jnp.bfloat16)
    return jnp.sum(expert_out * row_wts.T[:, :, None], axis=0)


def solution(mesh):
    tok_spec = P(('dp', 'ep'), None)
    expert_spec = P('ep', None, None)

    def local_fn(hidden, norm_gain, w_gate, w1_shared, w3_shared, w2_shared, w1_experts, w3_experts, w2_experts, topk_ids):
        normed = rms_norm(hidden, norm_gain)
        gate_wts = router_weights(normed, w_gate, topk_ids)
        shared_out = swiglu(normed, w1_shared, w3_shared, w2_shared)
        all_rows = lax.all_gather(normed, 'ep', axis=0, tiled=True)
        all_ids = lax.all_gather(topk_ids, 'ep', axis=0, tiled=True)
        all_wts = lax.all_gather(gate_wts, 'ep', axis=0, tiled=True)
        local_count = w1_experts.shape[0]
        local_ids = lax.axis_index('ep') * local_count + jnp.arange(local_count)
        row_wts = jnp.sum(jnp.where(all_ids[:, :, None] == local_ids, all_wts[:, :, None], 0.0), axis=1)
        part_sum = routed_experts(all_rows, row_wts, w1_experts, w3_experts, w2_experts)
        routed = lax.psum_scatter(part_sum, 'ep', scatter_dimension=0, tiled=True)
        return (hidden.astype(jnp.float32) + shared_out.astype(jnp.float32) + routed).astype(jnp.bfloat16)

    return jax.shard_map(local_fn, mesh=mesh, in_specs=(tok_spec, P(), P(), P(), P(), P(), expert_spec, expert_spec, expert_spec, tok_spec), out_specs=tok_spec, check_vma=False)
```

profile of v0, /device:TPU:0, one launch (start us, length us, event | category | flops | bytes accessed | tf_op | source)
XLA Modules:
  0.0 265.4 jit_solution(4519859292168503410)
XLA Ops:
  6.5 0.7 convert_element_type.32
  7.3 1.2 fusion.12
  8.5 1.9 fusion.14
  10.4 0.0 all-gather.4.cloned.1.call-update
  10.4 0.0 reduce-scatter.2.cloned.1.call-start
  10.5 0.7 bitcast_or_fusion
  11.2 0.1 copy.39
  11.3 0.1 reshape.28
  11.4 1.3 fusion.25
  12.8 4.0 %gather_fusion = f32[576]{0:T(1024)S(1)} fusion(f32[96,64]{0,1:T(8,128)S(1)} %fusion.16, s32[576]{0:T(1024)S(1)} %reshape.28), kind=kCustom, calls=%fused_computation | custom fusion | bytes 9216 | tf_op jit(solution)/shard_map/jit(take_along_axis)/gather | solution.py:25
  16.9 0.1 reshape.31
  17.0 0.1 copy.40
  17.1 14.0 %all-gather.1 = f32[8,96,6]{1,2,0:T(8,128)S(1)} all-gather(f32[1,96,6]{1,2,0:T(8,128)S(1)} %multiply_bitcast_fusion), channel_id=1, replica_groups=mesh['dp'=1,'ep'=8] {'ep'}, dimensions={0}, use_global_device_ids=true | all-gather | bytes 20736 | tf_op jit(solution)/shard_map/all_gather | solution.py:46
  31.2 0.1 reshape.42
  31.2 11.2 %all-gather = s32[8,96,6]{1,2,0:T(8,128)S(1)} all-gather(s32[1,96,6]{1,2,0:T(8,128)S(1)} %bitcast.75), channel_id=1, replica_groups=mesh['dp'=1,'ep'=8] {'ep'}, dimensions={0}, use_global_device_ids=true | all-gather | bytes 20736 | tf_op jit(solution)/shard_map/all_gather | solution.py:45
  42.4 0.1 reshape.40
  42.5 0.7 select_reduce_fusion
  43.2 47.9 %fusion.5 = f32[768,8,1408]{2,0,1:T(8,128)} fusion(bf16[8,2048,1408]{2,1,0:T(8,128)(2,1)} %param.17, bf16[768,2048]{1,0:T(8,128)(2,1)} %all-gather.4.cloned.1.call-done), kind=kOutput, calls=%fused_computation.11 | convolution fusion | flops 35433480192 | bytes 83886080 | tf_op jit(solution)/shard_map/nd,edf->enf/dot_general | solution.py:30
  91.1 52.7 %fusion.51 = bf16[8,768,1408]{2,1,0:T(8,128)(2,1)} fusion(f32[768,8,1408]{2,0,1:T(8,128)} %fusion.5, bf16[8,2048,1408]{2,1,0:T(8,128)(2,1)} %param.16, bf16[768,2048]{1,0:T(8,128)(2,1)S(1)} %copy-done.9), kind=kOutput, calls=%bitcast_fusion.clone.1 | convolution fusion | flops 35485384704 | bytes 101187584 | tf_op jit(solution)/shard_map/nd,edf->enf/dot_general | solution.py:29
  143.8 49.4 %multiply_reduce_fusion = f32[768,2048]{1,0:T(8,128)} fusion(f32[8,768]{1,0:T(8,128)S(1)} %bitcast.76, bf16[8,1408,2048]{2,1,0:T(8,128)(2,1)} %param.18, bf16[8,768,1408]{2,1,0:T(8,128)(2,1)} %fusion.51), kind=kOutput, calls=%fused_computation.1 | convolution fusion | flops 35482238976 | bytes 69754880 | tf_op jit(solution)/shard_map/enf,efd->end/dot_general | solution.py:32
  193.2 0.0 reduce-scatter.2.cloned.1.call-update
  193.3 6.3 %fusion.23 = f32[96,2816]{1,0:T(8,128)S(1)} fusion(bf16[2048,2816]{1,0:T(8,128)(2,1)} %param.13, bf16[96,2048]{1,0:T(8,128)(2,1)S(1)} %copy-done.2, f32[2048]{0:T(1024)S(1)} %copy-done.4, f32[96]{0:T(128)S(1)} %copy-done.8), kind=kOutput, calls=%fused_computation.36 | convolution fusion | flops 1108082688 | bytes 13017472 | tf_op jit(solution)/shard_map/dot_general | solution.py:17
  199.6 46.5 %reduce-scatter.2.cloned.1.call-done = f32[96,2048]{1,0:T(8,128)} async-done(((f32[768,2048]{1,0:T(8,128)}), f32[96,2048]{1,0:T(8,128)}) %reduce-scatter.2.cloned.1.call-update) | async-done | bytes 786448 | tf_op jit(solution)/shard_map/reduce_scatter | solution.py:51
  246.1 12.4 %fusion.11 = bf16[96,2048]{1,0:T(8,128)(2,1)} fusion(f32[96,2048]{1,0:T(8,128)} %reduce-scatter.2.cloned.1.call-done, bf16[2816,2048]{1,0:T(8,128)(2,1)} %param.15, bf16[96,2048]{1,0:T(8,128)(2,1)S(1)} %copy-done.2, bf16[2048,2816]{1,0:T(8,128)(2,1)} %param.14, f32[96,2816]{1,0:T(8,128)S(1)} %fusion.23, f32[2048]{0:T(1024)S(1)} %copy-done.4, ...), kind=kOutput, calls=%fused_computation.18 | convolution fusion | flops 2218180608 | bytes 25731456 | tf_op jit(solution)/shard_map/dot_general | solution.py:20
  (29 shorter events, 0.1 us)
Async XLA Ops:
  6.5 4.9 %copy-start = (bf16[2048,64]{0,1:T(8,128)(2,1)S(1)}, bf16[2048,64]{0,1:T(8,128)(2,1)}, u32[]{:S(2)}) copy-start(bf16[2048,64]{0,1:T(8,128)(2,1)} %param.12) | copy-start | bytes 786436
  6.5 36.7 %all-gather.4.cloned.1.call-start = ((), (), s32[]{:S(2)}) async-start(), calls=%async_computation.1 | async-start | bytes 3538944 | tf_op jit(solution)/shard_map/all_gather | solution.py:44
  7.3 9.6 %copy-start.3 = (f32[2048]{0:T(1024)}, f32[2048]{0:T(1024)S(1)}, u32[]{:S(2)}) copy-start(f32[2048]{0:T(1024)S(1)} %convert_element_type.32) | copy-start | bytes 24580
  8.5 8.4 %copy-start.7 = (f32[96]{0:T(128)}, f32[96]{0:T(128)S(1)}, u32[]{:S(2)}) copy-start(f32[96]{0:T(128)S(1)} %add_rsqrt_fusion) | copy-start | bytes 1156
  10.4 235.7 %reduce-scatter.2.cloned.1.call-start = ((), (), s32[]{:S(2)}) async-start(), calls=%async_computation.2 | async-start | bytes 7077888 | tf_op jit(solution)/shard_map/reduce_scatter | solution.py:51
  12.8 4.3 %copy-start.5 = (s32[96,6]{0,1:T(8,128)S(1)}, s32[96,6]{0,1:T(8,128)}, u32[]{:S(2)}) copy-start(s32[96,6]{0,1:T(8,128)} %param.19) | copy-start | bytes 6916
  43.2 47.9 %copy-start.9 = (bf16[768,2048]{1,0:T(8,128)(2,1)S(1)}, bf16[768,2048]{1,0:T(8,128)(2,1)}, u32[]{:S(2)}) copy-start(bf16[768,2048]{1,0:T(8,128)(2,1)} %all-gather.4.cloned.1.call-done) | copy-start | bytes 9437188
  91.1 52.7 %copy-start.6 = (f32[768,8]{0,1:T(8,128)S(1)}, f32[768,8]{0,1:T(8,128)}, u32[]{:S(2)}) copy-start(f32[768,8]{0,1:T(8,128)} %select_reduce_fusion) | copy-start | bytes 73732
  143.8 49.4 %copy-start.2 = (bf16[96,2048]{1,0:T(8,128)(2,1)S(1)}, bf16[96,2048]{1,0:T(8,128)(2,1)}, u32[]{:S(2)}) copy-start(bf16[96,2048]{1,0:T(8,128)(2,1)} %param.10) | copy-start | bytes 1179652
  143.8 49.4 %copy-start.4 = (f32[2048]{0:T(1024)S(1)}, f32[2048]{0:T(1024)}, u32[]{:S(2)}) copy-start(f32[2048]{0:T(1024)} %copy-done.3) | copy-start | bytes 24580
  143.8 49.4 %copy-start.8 = (f32[96]{0:T(128)S(1)}, f32[96]{0:T(128)}, u32[]{:S(2)}) copy-start(f32[96]{0:T(128)} %copy-done.7) | copy-start | bytes 1156
  193.2 65.3 %copy-start.1 = (bf16[2048,64]{0,1:T(8,128)(2,1)S(1)}, bf16[2048,64]{0,1:T(8,128)(2,1)}, u32[]{:S(2)}) copy-start(bf16[2048,64]{0,1:T(8,128)(2,1)} %param.12) | copy-start | bytes 786436
Sparse Core Ops, SparseCore 0:
  10.5 29.8 all-gather.3
  193.3 52.7 reduce-scatter.1
where the time goes:
time: 266 us; the launch traced here: 265 us
  matrix products  170 us (64%)
  waiting for transfers between devices  46.5 us (17%)
  blocking collectives  25.2 us (9%)
  between operations  13.6 us (5%)
  other arithmetic  5.27 us (2%)
  local copies, waits for them, and re-layouts  4.68 us (2%)
    dot_general x1, matrix products, routed_experts(): jnp.einsum('nd,edf->enf', rows_in, w1_experts, preferred_element_type=jnp...  52.7 us
    dot_general x1, matrix products, routed_experts(): jnp.einsum('enf,efd->end', inner_act, w2_experts, preferred_element_type=...  49.4 us
    dot_general x1, matrix products, routed_experts(): jnp.einsum('nd,edf->enf', rows_in, w3_experts, preferred_element_type=jnp...  47.9 us
    reduce_scatter x1, waiting for transfers between devices, local_fn(): routed = lax.psum_scatter(part_sum, 'ep', scatter_dimension=0, tiled=True)  46.5 us
    all_gather x1, blocking collectives, local_fn(): all_wts = lax.all_gather(gate_wts, 'ep', axis=0, tiled=True)  14 us
    dot_general x1, matrix products, swiglu(): jnp.dot(inner_act, w_down, preferred_element_type=jnp.float32)  12.4 us
    all_gather x1, blocking collectives, local_fn(): all_ids = lax.all_gather(topk_ids, 'ep', axis=0, tiled=True)  11.2 us
    dot_general x1, matrix products, swiglu(): gate_act = jnp.dot(rows_in, w_up, preferred_element_type=jnp.float32)  6.35 us
  transfers between devices with their start and end apart: 2, of which 1 were waited for; matrix products, arithmetic and copies ran while one was open for 5% of the time, Pallas kernels for 0%

commit v1 on v0

v1 whole, which is shorter than its diff:
```python
import functools

import jax
import jax.numpy as jnp
from jax import lax
from jax.experimental import pallas as pl
from jax.experimental.pallas import tpu as pltpu
from jax.sharding import PartitionSpec as P

ROUTE_SCALE = 16
NORM_EPS = 1e-6
CAP = 128
CHUNK = 256
RING = 3
F32 = jnp.float32
BF16 = jnp.bfloat16


def dot_f32(lhs, rhs):
    return jnp.dot(lhs, rhs, preferred_element_type=F32)


def moe_kernel(base_ref, gain_ref, wgt_ref, idst_ref, y_hbm, w1s, w3s, w2s, w1e, w3e, w2e,
               out_ref, load_ref,
               y_ref, slots, ball, vall, vt_ref, rk_ref, tr_ref, q_all, xg_ref, act_ref, act_s,
               pbuf, dbuf, abuf, rbuf, sbuf,
               y_sem, wsem, ssem, rsem, ds_sem, dr_sem, as_sem, ar_sem, bs_sem, br_sem):
    rows = y_ref.shape[0]
    half = rows // 2
    experts, _, ff = w1e.shape
    chunks = w2e.shape[2] // CHUNK
    tokens = rows * 8
    me = lax.axis_index("ep")
    core = me % 2
    chip = me // 2
    xpos = chip % 2
    ypos = chip // 2
    partner = me + 1 - 2 * core
    xdev = me + 2 - 4 * xpos
    ydev = me + 4 - 8 * ypos
    xq = chip + 1 - 2 * xpos
    yq = chip + 2 - 4 * ypos
    dq = 3 - chip
    my_pos = core * 4 + chip
    x_pos = core * 4 + xq
    y_pos = core * 4 + yq
    d_pos = core * 4 + dq

    def issue_shared(part, s):
        cols = pl.ds(part * ff, ff)
        pltpu.make_async_copy(w1s.at[:, cols], slots.at[s, 0], wsem.at[s, 0]).start()
        pltpu.make_async_copy(w3s.at[:, cols], slots.at[s, 1], wsem.at[s, 1]).start()

    def issue_expert(e, s):
        pltpu.make_async_copy(w1e.at[e], slots.at[s, 0], wsem.at[s, 0]).start()
        pltpu.make_async_copy(w3e.at[e], slots.at[s, 1], wsem.at[s, 1]).start()

    def issue_down(c, s):
        cols = pl.ds(pl.multiple_of(c * CHUNK, CHUNK), CHUNK)
        for j in range(10):
            h, k = j // 5, j % 5
            src = w2e.at[j, :, cols] if j < experts else w2s.at[pl.ds((j - experts) * ff, ff), cols]
            dst = slots.at[s, h, pl.ds(0, ff), pl.ds(k * CHUNK, CHUNK)]
            pltpu.make_async_copy(src, dst, wsem.at[s, h]).start()

    def wait_full(s, h):
        pltpu.make_async_copy(w1e.at[0], slots.at[s, h], wsem.at[s, h]).wait()

    def wait_down(s, h):
        box = (pl.ds(0, ff), pl.ds(0, 5 * CHUNK))
        pltpu.make_async_copy(w1e.at[(0,) + box], slots.at[(s, h) + box], wsem.at[s, h]).wait()

    def up_project(lhs, s, dst, off):
        start = 0
        while start < ff:
            width = min(CHUNK, ff - start)
            cols = slice(start, start + width)
            gate = dot_f32(lhs[...], slots[s, 0, :, cols])
            lin = dot_f32(lhs[...], slots[s, 1, :, cols])
            dst[:, off + start:off + start + width] = (jax.nn.silu(gate) * lin).astype(BF16)
            start += width

    y_copy = pltpu.make_async_copy(y_hbm, y_ref, y_sem)
    y_copy.start()
    issue_shared(0, 0)
    issue_shared(1, 1)
    issue_expert(0, 2)

    barrier = pltpu.get_barrier_semaphore()
    for dev in (partner, xdev, ydev):
        pl.semaphore_signal(barrier, inc=1, device_id={"ep": dev}, device_id_type=pl.DeviceIdType.MESH)

    y_copy.wait()
    rows_f = y_ref[...].astype(F32)
    inv_rms = lax.rsqrt(jnp.mean(rows_f * rows_f, axis=-1, keepdims=True) + NORM_EPS)
    ball[my_pos] = (rows_f * inv_rms * gain_ref[...].astype(F32)).astype(BF16)
    pl.semaphore_wait(barrier, 3)

    def remote(t, src, dst, dev):
        return pltpu.make_async_remote_copy(
            src_ref=src, dst_ref=dst, send_sem=ssem.at[t], recv_sem=rsem.at[t],
            device_id={"ep": dev}, device_id_type=pl.DeviceIdType.MESH)

    def block(pos, h=None):
        return ball.at[pos] if h is None else ball.at[pos, pl.ds(h * half, half)]

    def same(t, ref, dev):
        return remote(t, ref, ref, dev)

    x_h0 = same(0, block(my_pos, 0), xdev)
    y_h1 = same(1, block(my_pos, 1), ydev)
    x_h1 = same(2, block(my_pos, 1), xdev)
    y_h0 = same(3, block(my_pos, 0), ydev)
    p_own = same(4, block(my_pos), partner)
    for cp in (x_h0, y_h1, x_h1, y_h0, p_own):
        cp.start()

    logits = lax.dot_general(wgt_ref[...], ball[my_pos], (((1,), (1,)), ((), ())), preferred_element_type=F32)
    expv = jnp.exp(logits - jnp.max(logits, axis=0, keepdims=True))
    probs = expv / jnp.sum(expv, axis=0, keepdims=True)
    eid = lax.broadcasted_iota(jnp.int32, logits.shape, 0)
    chosen = idst_ref[0:1, :] == eid
    for j in range(1, idst_ref.shape[0]):
        chosen = jnp.logical_or(chosen, idst_ref[j:j + 1, :] == eid)
    vall[my_pos] = jnp.full(vall.shape[1:], -1.0, F32)
    vall[my_pos, :, 0:rows] = jnp.where(chosen, ROUTE_SCALE * probs, -1.0)

    x_v = same(5, vall.at[my_pos], xdev)
    y_v = same(6, vall.at[my_pos], ydev)
    p_v = same(7, vall.at[my_pos], partner)
    for cp in (x_v, y_v, p_v):
        cp.start()

    wait_full(0, 0)
    wait_full(0, 1)
    up_project(ball.at[my_pos], 0, act_s, 0)
    issue_expert(1, 0)

    x_h0.wait_recv()
    f_h0 = same(8, block(x_pos, 0), ydev)
    f_h0.start()
    y_h1.wait_recv()
    f_h1 = same(9, block(y_pos, 1), xdev)
    f_h1.start()
    x_v.wait_recv()
    f_v = same(10, vall.at[x_pos], ydev)
    f_v.start()
    y_v.wait_recv()
    p_xv = same(11, vall.at[x_pos], partner)
    p_yv = same(12, vall.at[y_pos], partner)
    p_xv.start()
    p_yv.start()

    wait_full(1, 0)
    wait_full(1, 1)
    up_project(ball.at[my_pos], 1, act_s, ff)
    issue_expert(2, 1)

    upper = lax.broadcasted_iota(jnp.int32, (tokens, tokens), 0) < lax.broadcasted_iota(jnp.int32, (tokens, tokens), 1)
    upper = jnp.where(upper, 1.0, 0.0).astype(BF16)

    x_h1.wait_recv()
    p_x = same(13, block(x_pos), partner)
    p_x.start()
    y_h0.wait_recv()
    p_y = same(14, block(y_pos), partner)
    p_y.start()
    f_v.wait_recv()
    p_dv = same(15, vall.at[d_pos], partner)
    p_dv.start()
    f_h0.wait_recv()
    p_d0 = same(16, block(d_pos, 0), partner)
    p_d0.start()
    f_h1.wait_recv()
    p_d1 = same(17, block(d_pos, 1), partner)
    p_d1.start()
    for cp in (p_v, p_xv, p_yv, p_dv):
        cp.wait_recv()

    for k in range(8):
        vt_ref[:, k * rows:(k + 1) * rows] = vall[k, :, 0:rows]
    counts = jnp.sum(jnp.where(vt_ref[...] > -0.5, 1.0, 0.0), axis=1, keepdims=True)
    load_ref[...] = jnp.broadcast_to(jnp.max(counts, axis=0, keepdims=True), load_ref.shape)
    v_loc = vt_ref[pl.ds(pl.multiple_of(me * experts, experts), experts), :]
    sel = v_loc > -0.5
    picks = jnp.where(sel, 1.0, 0.0)
    picks = jnp.concatenate([picks, picks], axis=0).astype(BF16)
    rank = dot_f32(picks, upper)[0:experts] - base_ref[0:1, 0:1]
    rank = jnp.where(sel, rank, -1.0)
    rk_ref[...] = rank
    stacked = jnp.concatenate(
        [rank, jnp.where(sel, v_loc, 0.0), jnp.zeros((128 - 2 * experts, tokens), F32)], axis=0)
    tr_ref[...] = stacked.T
    lane = lax.broadcasted_iota(jnp.int32, (tokens, CAP), 1).astype(F32)
    for e in range(experts):
        q_all[e] = jnp.where(tr_ref[:, e:e + 1] == lane, 1.0, 0.0).astype(BF16)

    for cp in (p_own, p_x, p_y, p_d0, p_d1):
        cp.wait_recv()

    slot_row = lax.broadcasted_iota(jnp.int32, (CAP, tokens), 0).astype(F32)

    def stage_one(e, carry):
        s = (e + 2) % RING
        pick = jnp.where(rk_ref[pl.ds(e, 1), :] == slot_row, 1.0, 0.0).astype(BF16)
        for k in range(0, ball.shape[2], 512):
            xg_ref[:, k:k + 512] = dot_f32(pick, ball[:, :, k:k + 512].reshape(tokens, 512)).astype(BF16)
        wait_full(s, 0)
        wait_full(s, 1)
        up_project(xg_ref, s, act_ref.at[e], 0)

        @pl.when(e + RING < experts)
        def _():
            issue_expert(e + RING, s)

        @pl.when(e + RING >= experts)
        def _():
            issue_down(e + RING - experts, s)

        return carry

    lax.fori_loop(0, experts, stage_one, 0)

    def send_d(c):
        return pltpu.make_async_remote_copy(
            src_ref=pbuf.at[c, 1 - core], dst_ref=dbuf.at[c], send_sem=ds_sem.at[c], recv_sem=dr_sem.at[c],
            device_id={"ep": partner}, device_id_type=pl.DeviceIdType.MESH)

    def send_a(c, i):
        return pltpu.make_async_remote_copy(
            src_ref=pbuf.at[c, core, dq, pl.ds(i * half, half)], dst_ref=abuf.at[c, i],
            send_sem=as_sem.at[c, i], recv_sem=ar_sem.at[c, i],
            device_id={"ep": (xdev, ydev)[i]}, device_id_type=pl.DeviceIdType.MESH)

    def send_b(c, i):
        return pltpu.make_async_remote_copy(
            src_ref=pbuf.at[c, core, (xq, yq)[i]], dst_ref=rbuf.at[c, i],
            send_sem=bs_sem.at[c, i], recv_sem=br_sem.at[c, i],
            device_id={"ep": (xdev, ydev)[i]}, device_id_type=pl.DeviceIdType.MESH)

    def compute_chunk(c):
        s = (c + experts + 2) % RING
        wait_down(s, 0)
        wait_down(s, 1)
        total = None
        for e in range(experts):
            slab = slots[s, e // 5, 0:ff, (e % 5) * CHUNK:(e % 5 + 1) * CHUNK]
            res = dot_f32(act_ref[e], slab).astype(BF16)
            part = tr_ref[:, experts + e:experts + e + 1] * dot_f32(q_all[e], res)
            part = part.reshape(pbuf.shape[1:])
            if e == 0:
                pbuf[c] = part
            else:
                pbuf[c] = pbuf[c] + part
        lo = slots[s, 1, 0:ff, 3 * CHUNK:4 * CHUNK]
        hi = slots[s, 1, 0:ff, 4 * CHUNK:5 * CHUNK]
        sbuf[c] = (dot_f32(act_s[:, 0:ff], lo) + dot_f32(act_s[:, ff:2 * ff], hi)).astype(BF16)

        @pl.when(c + RING < chunks)
        def _():
            issue_down(c + RING, s)

        send_d(c).start()

    def reduce_pair(c):
        send_d(c).wait_recv()
        pbuf[c, core] = pbuf[c, core] + dbuf[c]
        send_a(c, 0).start()
        send_a(c, 1).start()

    def reduce_diag(c):
        send_a(c, 0).wait_recv()
        pbuf[c, core, yq, 0:half] = pbuf[c, core, yq, 0:half] + abuf[c, 0]
        send_b(c, 1).start()
        send_a(c, 1).wait_recv()
        pbuf[c, core, xq, half:rows] = pbuf[c, core, xq, half:rows] + abuf[c, 1]
        send_b(c, 0).start()

    def finish(c):
        cols = pl.ds(pl.multiple_of(c * CHUNK, CHUNK), CHUNK)
        local = y_ref[:, cols].astype(F32) + sbuf[c].astype(F32)
        local = jnp.where(base_ref[0:1, 0:1] == 0.0, local, 0.0)
        send_b(c, 0).wait_recv()
        send_b(c, 1).wait_recv()
        out_ref[:, cols] = local + (pbuf[c, core, chip] + rbuf[c, 0] + rbuf[c, 1])

    def stage_two(c, carry):
        pl.when(c < chunks)(lambda: compute_chunk(c))
        pl.when(jnp.logical_and(c >= 1, c < chunks + 1))(lambda: reduce_pair(c - 1))
        pl.when(jnp.logical_and(c >= 2, c < chunks + 2))(lambda: reduce_diag(c - 2))
        pl.when(c >= 3)(lambda: finish(c - 3))
        return carry

    lax.fori_loop(0, chunks + 3, stage_two, 0)

    for cp in (x_h0, y_h1, x_h1, y_h0, p_own, x_v, y_v, p_v, f_h0, f_h1, f_v, p_xv, p_yv, p_x, p_y, p_dv, p_d0, p_d1):
        cp.wait_send()

    def drain(c, carry):
        send_d(c).wait_send()
        for i in range(2):
            send_a(c, i).wait_send()
            send_b(c, i).wait_send()
        return carry

    lax.fori_loop(0, chunks, drain, 0)


def moe_call(base, gain, wgt, idst, y, w1s, w3s, w2s, w1e, w3e, w2e):
    rows, width = y.shape
    experts, _, ff = w1e.shape
    all_experts = wgt.shape[0]
    tokens = rows * 8
    chunks = width // CHUNK
    vmem = pl.BlockSpec(memory_space=pltpu.VMEM)
    hbm = pl.BlockSpec(memory_space=pl.ANY)
    dma = pltpu.SemaphoreType.DMA
    return pl.pallas_call(
        moe_kernel,
        out_shape=(jax.ShapeDtypeStruct((rows, width), F32), jax.ShapeDtypeStruct((8, 128), F32)),
        in_specs=[vmem] * 4 + [hbm] * 7,
        out_specs=(vmem, vmem),
        scratch_shapes=[
            pltpu.VMEM((rows, width), BF16),
            pltpu.VMEM((RING, 2, width, ff), BF16),
            pltpu.VMEM((8, rows, width), BF16),
            pltpu.VMEM((8, all_experts, 128), F32),
            pltpu.VMEM((all_experts, tokens), F32),
            pltpu.VMEM((experts, tokens), F32),
            pltpu.VMEM((tokens, 128), F32),
            pltpu.VMEM((experts, tokens, CAP), BF16),
            pltpu.VMEM((CAP, width), BF16),
            pltpu.VMEM((experts, CAP, ff), BF16),
            pltpu.VMEM((rows, 2 * ff), BF16),
            pltpu.VMEM((chunks, 2, 4, rows, CHUNK), F32),
            pltpu.VMEM((chunks, 4, rows, CHUNK), F32),
            pltpu.VMEM((chunks, 2, rows // 2, CHUNK), F32),
            pltpu.VMEM((chunks, 2, rows, CHUNK), F32),
            pltpu.VMEM((chunks, rows, CHUNK), BF16),
            dma,
            dma((RING, 2)),
            dma((18,)),
            dma((18,)),
            dma((chunks,)),
            dma((chunks,)),
            dma((chunks, 2)),
            dma((chunks, 2)),
            dma((chunks, 2)),
            dma((chunks, 2)),
        ],
        compiler_params=pltpu.CompilerParams(
            collective_id=0, has_side_effects=True, vmem_limit_bytes=67_000_000),
    )(base, gain, wgt, idst, y, w1s, w3s, w2s, w1e, w3e, w2e)


def solution(mesh):
    tok_spec = P(('dp', 'ep'), None)
    expert_spec = P('ep', None, None)

    def local_fn(hidden, norm_gain, w_gate, w1_shared, w3_shared, w2_shared, w1_experts, w3_experts, w2_experts, topk_ids):
        def routed_round(base):
            return moe_call(base, norm_gain[None, :], w_gate.T, topk_ids.T, hidden, w1_shared, w3_shared, w2_shared,
                            w1_experts, w3_experts, w2_experts)

        total, load = routed_round(jnp.zeros((8, 128), F32))

        def more(state):
            return state[0] < load[0, 0]

        def body(state):
            start, acc = state
            part, _ = routed_round(jnp.full((8, 128), start, F32))
            return start + CAP, acc + part

        total = lax.while_loop(more, body, (jnp.float32(CAP), total))[1]
        return total.astype(BF16)

    return jax.shard_map(local_fn, mesh=mesh, in_specs=(tok_spec, P(), P(), P(), P(), P(), expert_spec, expert_spec, expert_spec, tok_spec), out_specs=tok_spec, check_vma=False)
```

time: 266 us -> 97.9 us (0.37)
  matrix products: 170 us -> 0 us
  Pallas kernels: 0 us -> 91.8 us
  waiting for transfers between devices: 46.5 us -> 0 us
  blocking collectives: 25.2 us -> 0 us
  between operations: 13.6 us -> 0.04 us
  other arithmetic: 5.27 us -> 1.92 us
    dot_general x6 -> x0, matrix products: 170 us -> none  [the longest x1 52.7 us: routed_experts(): jnp.einsum('nd,edf->enf', rows_in, w1_experts, preferred_element_type=jnp...]
    pallas_call x0 -> x1, Pallas kernels: none -> 91.8 us  [moe_call(): pl.pallas_call(moe_kernel, out_shape=(jax.ShapeDtypeStruct((rows, width),...]
    reduce_scatter x1 -> x0, waiting for transfers between devices: 46.5 us -> none  [local_fn(): routed = lax.psum_scatter(part_sum, 'ep', scatter_dimension=0, tiled=True)]
    all_gather x2 -> x0, blocking collectives: 25.2 us -> none  [the longest x1 14 us: local_fn(): all_wts = lax.all_gather(gate_wts, 'ep', axis=0, tiled=True)]
    gather x5 -> x0, local copies, waits for them, and re-layouts: 4.47 us -> none  [router_weights(): return ROUTE_SCALE * jnp.take_along_axis(gate_probs, topk_ids, axis=1)]
  transfers between devices with their start and end apart: 2 -> 0, of which waited for: 1 -> 0; matrix products, arithmetic and copies ran while one was open for 5% -> 0% of each run, Pallas kernels for 0% -> 0%
where the time goes in v1:
time: 97.9 us; the launch traced here: 97.7 us
  Pallas kernels  91.8 us (94%)
  local copies, waits for them, and re-layouts  3.08 us (3%)
  other arithmetic  1.92 us (2%)
    pallas_call x1, Pallas kernels, moe_call(): pl.pallas_call(moe_kernel, out_shape=(jax.ShapeDtypeStruct((rows, width),...  91.8 us

profile of v1, /device:TPU:0, one launch (start us, length us, event | category | flops | bytes accessed | tf_op | source)
XLA Modules:
  0.0 97.7 jit_solution(10467368168865962261)
XLA Ops:
  0.0 1.3 %broadcast_in_dim.13.gain_ref = bf16[1,2048]{1,0:T(2,128)(2,1)} reshape(bf16[2048]{0:T(1024)(128)(2,1)} %param.13) | data formatting | bytes 8192 | tf_op jit(solution)/shard_map/broadcast_in_dim | solution.py:362
  1.3 0.6 broadcast_in_dim.12.base_ref
  1.9 0.0 copy-start
  1.9 0.0 copy-start.1
  1.9 91.8 %shard_map.100 = (f32[96,2048]{1,0:T(8,128)}, f32[8,128]{1,0:T(8,128)}) custom-call(f32[8,128]{1,0:T(8,128)} %broadcast_in_dim.12.base_ref, bf16[1,2048]{1,0:T(2,128)(2,1)} %broadcast_in_dim.13.gain_ref, bf16[64,2048]{1,0:T(8,128)(2,1)} %bitcast.10, s32[6,96]{1,0:T(8,128)} %bitcast.12, bf16[96,2048]{1,0:T(8,128)(2,1)} %y_hbm.1, bf16[2048,2816]{1,0:T(8,128)(2,1)} %w1s.1, ...), custom_call_target="tpu_custom_call" | custom-call | tf_op jit(solution)/shard_map/pallas_call | solution.py:318
  93.7 0.0 copy-done
  93.7 0.0 copy-done.1
  93.7 2.0 %while.10 = (f32[]{:T(128)}, f32[96,2048]{1,0:T(8,128)}, f32[8,128]{1,0:T(8,128)}, bf16[2048]{0:T(1024)(128)(2,1)S(1)}, bf16[2048,64]{0,1:T(8,128)(2,1)}, /*inde...) while((f32[]{:T(128)}, f32[96,2048]{1,0:T(8,128)}, ...), condition=%wide.region_1.0_spmd, body=%wide.region_0.0_spmd.sunk | while | flops 196610 | bytes 2371737 | solution.py:375
  93.7 1.2 %slice.3 = f32[1,1]{1,0:T(1,128)} slice(f32[8,128]{1,0:T(8,128)} %get-tuple-element.119), slice={[0:1], [0:1]} | slice | bytes 8 | tf_op jit(solution)/shard_map/while/cond/slice | solution.py:368
  95.8 1.9 %convert_element_type.3 = bf16[96,2048]{1,0:T(8,128)(2,1)} convert(f32[96,2048]{1,0:T(8,128)} %get-tuple-element.78) | non-fusion elementwise | flops 196608 | bytes 1179648 | tf_op jit(solution)/shard_map/convert_element_type | solution.py:376
Async XLA Ops:
  1.9 91.8 %copy-start = (s32[96,6]{0,1:T(8,128)S(1)}, s32[96,6]{0,1:T(8,128)}, u32[]{:S(2)}) copy-start(s32[96,6]{0,1:T(8,128)} %param.21) | copy-start | bytes 6916
  1.9 91.8 %copy-start.1 = (bf16[2048]{0:T(1024)(128)(2,1)S(1)}, bf16[2048]{0:T(1024)(128)(2,1)}, u32[]{:S(2)}) copy-start(bf16[2048]{0:T(1024)(128)(2,1)} %param.13) | copy-start | bytes 12292

commit v2 on v1

v2 whole, which is shorter than its diff:
```python
import functools

import jax
import jax.numpy as jnp
from jax import lax
from jax.experimental import pallas as pl
from jax.experimental.pallas import tpu as pltpu
from jax.sharding import PartitionSpec as P

ROUTE_SCALE = 16
NORM_EPS = 1e-6
CAP = 128
CHUNK = 256
RING = 4
WIDE = 512
F32 = jnp.float32
BF16 = jnp.bfloat16


def dot_f32(lhs, rhs):
    return jnp.dot(lhs, rhs, preferred_element_type=F32)


def moe_kernel(first, *refs):
    if first:
        base = 0.0
    else:
        base, refs = refs[0][0:1, 0:1], refs[1:]
    (gain_ref, wgt_ref, idst_ref, y_ref, w1s, w3s, w2s, w1e, w3e, w2e,
     out_hbm, load_hbm,
     out_ref, load_ref, slots, ball, vall, vt_ref, rk_ref, tr_ref, q_all, xg_ref, act_ref, act_s,
     pbuf, obuf, dbuf, abuf, rbuf, s_ref, e_ref,
     out_sem, load_sem, wsem, ssem, rsem, ds_sem, dr_sem, as_sem, ar_sem, bs_sem, br_sem) = refs
    rows = y_ref.shape[0]
    half = rows // 2
    experts, _, ff = w1e.shape
    picks_per_row = idst_ref.shape[0]
    chunks = w2e.shape[2] // CHUNK
    tokens = rows * 8
    me = lax.axis_index("ep")
    core = me % 2
    chip = me // 2
    xpos = chip % 2
    ypos = chip // 2
    partner = me + 1 - 2 * core
    xdev = me + 2 - 4 * xpos
    ydev = me + 4 - 8 * ypos
    xq = chip + 1 - 2 * xpos
    yq = chip + 2 - 4 * ypos
    dq = 3 - chip
    diag = 2 * dq + core

    def issue_shared(part, s):
        cols = pl.ds(part * ff, ff)
        pltpu.make_async_copy(w1s.at[:, cols], slots.at[s, 0], wsem.at[s, 0]).start()
        pltpu.make_async_copy(w3s.at[:, cols], slots.at[s, 1], wsem.at[s, 1]).start()

    def issue_expert(e, s):
        pltpu.make_async_copy(w1e.at[e], slots.at[s, 0], wsem.at[s, 0]).start()
        pltpu.make_async_copy(w3e.at[e], slots.at[s, 1], wsem.at[s, 1]).start()

    def issue_down(c, s):
        cols = pl.ds(pl.multiple_of(c * CHUNK, CHUNK), CHUNK)
        for j in range(experts + 2):
            h, k = j // 5, j % 5
            src = w2e.at[j, :, cols] if j < experts else w2s.at[pl.ds((j - experts) * ff, ff), cols]
            dst = slots.at[s, h, pl.ds(0, ff), pl.ds(k * CHUNK, CHUNK)]
            pltpu.make_async_copy(src, dst, wsem.at[s, h]).start()

    def wait_full(s, h):
        pltpu.make_async_copy(w1e.at[0], slots.at[s, h], wsem.at[s, h]).wait()

    def wait_down(s, h):
        box = (pl.ds(0, ff), pl.ds(0, 5 * CHUNK))
        pltpu.make_async_copy(w1e.at[(0,) + box], slots.at[(s, h) + box], wsem.at[s, h]).wait()

    def up_project(lhs, s, dst, off):
        body = ff // CHUNK * CHUNK
        rest = ff - body
        for start in range(0, body, CHUNK):
            cols = slice(start, start + CHUNK)
            gate = dot_f32(lhs[...], slots[s, 0, :, cols])
            lin = dot_f32(lhs[...], slots[s, 1, :, cols])
            dst[:, off + start:off + start + CHUNK] = (jax.nn.silu(gate) * lin).astype(BF16)
        both = jnp.concatenate([slots[s, 0, :, body:ff], slots[s, 1, :, body:ff]], axis=1)
        both = dot_f32(lhs[...], both)
        dst[:, off + body:off + ff] = (jax.nn.silu(both[:, 0:rest]) * both[:, rest:]).astype(BF16)

    barrier = pltpu.get_barrier_semaphore()
    for dev in (partner, xdev, ydev, diag):
        pl.semaphore_signal(barrier, inc=1, device_id={"ep": dev}, device_id_type=pl.DeviceIdType.MESH)
    issue_shared(0, 0)
    issue_shared(1, 1)
    issue_expert(0, 2)
    issue_expert(1, 3)

    rows_f = y_ref[...].astype(F32)
    inv_rms = lax.rsqrt(jnp.mean(rows_f * rows_f, axis=-1, keepdims=True) + NORM_EPS)
    ball[me] = (rows_f * inv_rms * gain_ref[...].astype(F32).reshape(1, y_ref.shape[1])).astype(BF16)
    logits = lax.dot_general(wgt_ref[...], ball[me], (((1,), (1,)), ((), ())), preferred_element_type=F32)
    expv = jnp.exp(logits - jnp.max(logits, axis=0, keepdims=True))
    probs = expv / jnp.sum(expv, axis=0, keepdims=True)
    eid = lax.broadcasted_iota(jnp.int32, logits.shape, 0)
    vall[me] = jnp.full(vall.shape[1:], -1.0, F32)
    for j in range(picks_per_row):
        ids = idst_ref[j:j + 1, :]
        vall[me, j:j + 1, 0:rows] = ids.astype(F32)
        weight = jnp.sum(jnp.where(ids == eid, probs, 0.0), axis=0, keepdims=True)
        vall[me, 8 + j:9 + j, 0:rows] = ROUTE_SCALE * weight
    pl.semaphore_wait(barrier, 4)

    def same(t, ref, dev):
        return pltpu.make_async_remote_copy(
            src_ref=ref, dst_ref=ref, send_sem=ssem.at[t], recv_sem=rsem.at[t],
            device_id={"ep": dev}, device_id_type=pl.DeviceIdType.MESH)

    def block(dev, h=None):
        return ball.at[dev] if h is None else ball.at[dev, pl.ds(h * half, half)]

    x_v = same(0, vall.at[me], xdev)
    y_v = same(1, vall.at[me], ydev)
    p_v = same(2, vall.at[me], partner)
    d_v = same(8, vall.at[me], diag)
    x_h0 = same(3, block(me, 0), xdev)
    y_h1 = same(4, block(me, 1), ydev)
    x_h1 = same(5, block(me, 1), xdev)
    y_h0 = same(6, block(me, 0), ydev)
    p_own = same(7, block(me), partner)
    for cp in (x_v, y_v, d_v, p_v, x_h0, y_h1, x_h1, y_h0, p_own):
        cp.start()
    p_xv = same(9, vall.at[xdev], partner)
    p_yv = same(10, vall.at[ydev], partner)
    p_dv = same(11, vall.at[diag], partner)
    f_h0 = same(12, block(xdev, 0), ydev)
    f_h1 = same(13, block(ydev, 1), xdev)
    p_x = same(14, block(xdev), partner)
    p_y = same(15, block(ydev), partner)
    p_d0 = same(16, block(diag, 0), partner)
    p_d1 = same(17, block(diag, 1), partner)

    wait_full(0, 0)
    wait_full(0, 1)
    up_project(ball.at[me], 0, act_s, 0)
    issue_expert(2, 0)
    x_v.wait_recv()
    p_xv.start()
    y_v.wait_recv()
    p_yv.start()
    d_v.wait_recv()
    p_dv.start()
    x_h0.wait_recv()
    f_h0.start()
    y_h1.wait_recv()
    f_h1.start()

    wait_full(1, 0)
    wait_full(1, 1)
    up_project(ball.at[me], 1, act_s, ff)
    issue_expert(3, 1)
    for cp in (p_v, p_xv, p_yv, p_dv):
        cp.wait_recv()

    for k in range(8):
        vt_ref[:, k * rows:(k + 1) * rows] = vall[k, :, 0:rows]
    all_experts = wgt_ref.shape[0]
    every = lax.broadcasted_iota(jnp.int32, (all_experts, tokens), 0).astype(F32)
    hits = jnp.zeros((all_experts, tokens), F32)
    for j in range(picks_per_row):
        hits = hits + jnp.where(vt_ref[j:j + 1, :] == every, 1.0, 0.0)
    load_ref[0, 0] = jnp.max(jnp.sum(hits, axis=1, keepdims=True))
    load_copy = pltpu.make_async_copy(load_ref, load_hbm, load_sem)
    load_copy.start()
    local = (lax.broadcasted_iota(jnp.int32, (experts, tokens), 0) + me * experts).astype(F32)
    picks = jnp.zeros((experts, tokens), F32)
    weights = jnp.zeros((experts, tokens), F32)
    for j in range(picks_per_row):
        match = vt_ref[j:j + 1, :] == local
        picks = jnp.where(match, 1.0, picks)
        weights = jnp.where(match, vt_ref[8 + j:9 + j, :], weights)
    sel = picks > 0.5
    picks = jnp.concatenate([picks, picks], axis=0).astype(BF16)
    upper = lax.broadcasted_iota(jnp.int32, (tokens, tokens), 0) < lax.broadcasted_iota(jnp.int32, (tokens, tokens), 1)
    upper = jnp.where(upper, 1.0, 0.0).astype(BF16)
    rank = dot_f32(picks, upper)[0:experts] - base
    rank = jnp.where(sel, rank, -1.0)
    rk_ref[0:experts, :] = rank
    rk_ref[experts:2 * experts, :] = weights

    x_h1.wait_recv()
    p_x.start()
    y_h0.wait_recv()
    p_y.start()

    stacked = jnp.concatenate([rk_ref[...], jnp.zeros((128 - 2 * experts, tokens), F32)], axis=0).T
    for k in range(8):
        pos = (k % 2) * 4 + k // 2
        tr_ref[pos * rows:(pos + 1) * rows, :] = stacked[k * rows:(k + 1) * rows, :]
    lane = lax.broadcasted_iota(jnp.int32, (tokens, CAP), 1).astype(F32)
    for e in range(experts):
        q_all[e] = jnp.where(tr_ref[:, e:e + 1] == lane, 1.0, 0.0).astype(BF16)

    f_h0.wait_recv()
    p_d0.start()
    f_h1.wait_recv()
    p_d1.start()
    for cp in (p_own, p_x, p_y, p_d0, p_d1):
        cp.wait_recv()

    slot_row = lax.broadcasted_iota(jnp.int32, (CAP, tokens), 0).astype(F32)
    width = ball.shape[2]

    def stage_one(e, carry):
        s = (e + 2) % RING
        pick = jnp.where(rk_ref[pl.ds(e, 1), :] == slot_row, 1.0, 0.0).astype(BF16)
        for k in range(0, width, WIDE):
            xg_ref[:, k:k + WIDE] = dot_f32(pick, ball[:, :, k:k + WIDE].reshape(tokens, WIDE)).astype(BF16)
        wait_full(s, 0)
        wait_full(s, 1)
        up_project(xg_ref, s, act_ref.at[e], 0)

        @pl.when(e + RING < experts)
        def _():
            issue_expert(e + RING, s)

        @pl.when(e + RING >= experts)
        def _():
            issue_down(e + RING - experts, s)

        return carry

    lax.fori_loop(0, experts, stage_one, 0)

    for cp in (x_v, y_v, d_v, p_v, x_h0, y_h1, x_h1, y_h0, p_own, p_xv, p_yv, p_dv, f_h0, f_h1, p_x, p_y, p_d0, p_d1):
        cp.wait_send()

    load_copy.wait()

    def send_d(c):
        return pltpu.make_async_remote_copy(
            src_ref=obuf.at[c % 2], dst_ref=dbuf.at[c % 2], send_sem=ds_sem.at[c], recv_sem=dr_sem.at[c],
            device_id={"ep": partner}, device_id_type=pl.DeviceIdType.MESH)

    def send_a(c, i):
        return pltpu.make_async_remote_copy(
            src_ref=pbuf.at[c, dq, pl.ds(i * half, half)], dst_ref=abuf.at[c, i],
            send_sem=as_sem.at[c, i], recv_sem=ar_sem.at[c, i],
            device_id={"ep": (xdev, ydev)[i]}, device_id_type=pl.DeviceIdType.MESH)

    def send_b(c, i, h):
        return pltpu.make_async_remote_copy(
            src_ref=pbuf.at[c, (xq, yq)[i], pl.ds(h * half, half)], dst_ref=rbuf.at[c, i, h],
            send_sem=bs_sem.at[c, i, h], recv_sem=br_sem.at[c, i, h],
            device_id={"ep": (xdev, ydev)[i]}, device_id_type=pl.DeviceIdType.MESH)

    def out_copy(c):
        cols = pl.ds(pl.multiple_of(c * CHUNK, CHUNK), CHUNK)
        return pltpu.make_async_copy(out_ref.at[:, cols], out_hbm.at[:, cols], out_sem.at[c])

    def down_project(c):
        s = (c + experts + 2) % RING
        wait_down(s, 0)
        wait_down(s, 1)
        for e in range(experts):
            slab = slots[s, e // 5, 0:ff, (e % 5) * CHUNK:(e % 5 + 1) * CHUNK]
            e_ref[e] = dot_f32(act_ref[e], slab).astype(BF16)
        lo = slots[s, 1, 0:ff, 3 * CHUNK:4 * CHUNK]
        hi = slots[s, 1, 0:ff, 4 * CHUNK:5 * CHUNK]
        cols = pl.ds(pl.multiple_of(c * CHUNK, CHUNK), CHUNK)
        s_ref[:, cols] = (dot_f32(act_s[:, 0:ff], lo) + dot_f32(act_s[:, ff:2 * ff], hi)).astype(BF16)

        @pl.when(c + RING < chunks)
        def _():
            issue_down(c + RING, s)

    def combine_side(dst, slot, side):
        own = pl.ds(pl.multiple_of(side * (tokens // 2), tokens // 2), tokens // 2)
        for e in range(experts):
            part = tr_ref[own, experts + e:experts + e + 1] * dot_f32(q_all[e, own, :], e_ref[e])
            part = part.reshape(dst.shape[1:])
            if e == 0:
                dst[slot] = part
            else:
                dst[slot] = dst[slot] + part

    def combine(c):
        @pl.when(c >= 2)
        def _():
            send_d(c - 2).wait_send()

        combine_side(obuf, c % 2, 1 - core)
        send_d(c).start()
        combine_side(pbuf, c, core)

    def reduce_pair(c):
        send_d(c).wait_recv()
        pbuf[c] = pbuf[c] + dbuf[c % 2]
        for i in range(2):
            send_a(c, i).start()
        for i in range(2):
            send_b(c, i, i).start()

    def reduce_diag(c):
        for i in range(2):
            send_a(c, 1 - i).wait_recv()
            q = (xq, yq)[i]
            rest = slice((1 - i) * half, (2 - i) * half)
            pbuf[c, q, rest] = pbuf[c, q, rest] + abuf[c, 1 - i]
            send_b(c, i, 1 - i).start()

    def finish(c):
        cols = pl.ds(pl.multiple_of(c * CHUNK, CHUNK), CHUNK)
        local = y_ref[:, cols].astype(F32) + s_ref[:, cols].astype(F32)
        if not first:
            local = jnp.where(base == 0.0, local, 0.0)
        for h in range(2):
            part = slice(h * half, (h + 1) * half)
            routed = pbuf[c, chip, part]
            for i in range(2):
                send_b(c, i, h).wait_recv()
                routed = routed + rbuf[c, i, h]
            out_ref[part, cols] = (local[part] + routed).astype(out_ref.dtype)
        out_copy(c).start()

        @pl.when(c >= chunks - 2)
        def _():
            send_d(c).wait_send()

        for i in range(2):
            send_a(c, i).wait_send()
            for h in range(2):
                send_b(c, i, h).wait_send()

    def stage_two(c, carry):
        pl.when(c < chunks)(lambda: down_project(c))
        pl.when(jnp.logical_and(c >= 1, c < chunks + 1))(lambda: reduce_pair(c - 1))
        pl.when(c < chunks)(lambda: combine(c))
        pl.when(jnp.logical_and(c >= 2, c < chunks + 2))(lambda: reduce_diag(c - 2))
        pl.when(c >= 4)(lambda: finish(c - 4))
        return carry

    lax.fori_loop(0, chunks + 4, stage_two, 0)

    def drain(c, carry):
        out_copy(c).wait()
        return carry

    lax.fori_loop(0, chunks, drain, 0)


def moe_call(base, gain, wgt, idst, y, w1s, w3s, w2s, w1e, w3e, w2e):
    first = base is None
    rows, width = y.shape
    experts, _, ff = w1e.shape
    tokens = rows * 8
    chunks = width // CHUNK
    vmem = pl.BlockSpec(memory_space=pltpu.VMEM)
    hbm = pl.BlockSpec(memory_space=pl.ANY)
    dma = pltpu.SemaphoreType.DMA
    small = ([] if first else [base]) + [gain, wgt, idst]
    return pl.pallas_call(
        functools.partial(moe_kernel, first),
        out_shape=(jax.ShapeDtypeStruct((rows, width), BF16 if first else F32), jax.ShapeDtypeStruct((1, 1), F32)),
        in_specs=[vmem] * (len(small) + 1) + [hbm] * 6,
        out_specs=(hbm, hbm),
        scratch_shapes=[
            pltpu.VMEM((rows, width), BF16 if first else F32),
            pltpu.SMEM((1, 1), F32),
            pltpu.VMEM((RING, 2, width, ff), BF16),
            pltpu.VMEM((8, rows, width), BF16),
            pltpu.VMEM((8, 16, 128), F32),
            pltpu.VMEM((16, tokens), F32),
            pltpu.VMEM((2 * experts, tokens), F32),
            pltpu.VMEM((tokens, 128), F32),
            pltpu.VMEM((experts, tokens, CAP), BF16),
            pltpu.VMEM((CAP, width), BF16),
            pltpu.VMEM((experts, CAP, ff), BF16),
            pltpu.VMEM((rows, 2 * ff), BF16),
            pltpu.VMEM((chunks, 4, rows, CHUNK), F32),
            pltpu.VMEM((2, 4, rows, CHUNK), F32),
            pltpu.VMEM((2, 4, rows, CHUNK), F32),
            pltpu.VMEM((chunks, 2, rows // 2, CHUNK), F32),
            pltpu.VMEM((chunks, 2, 2, rows // 2, CHUNK), F32),
            pltpu.VMEM((rows, width), BF16),
            pltpu.VMEM((experts, CAP, CHUNK), BF16),
            dma((chunks,)),
            dma,
            dma((RING, 2)),
            dma((18,)),
            dma((18,)),
            dma((chunks,)),
            dma((chunks,)),
            dma((chunks, 2)),
            dma((chunks, 2)),
            dma((chunks, 2, 2)),
            dma((chunks, 2, 2)),
        ],
        compiler_params=pltpu.CompilerParams(
            collective_id=0 if first else 1, has_side_effects=True, vmem_limit_bytes=67_000_000),
    )(*small, y, w1s, w3s, w2s, w1e, w3e, w2e)


def solution(mesh):
    tok_spec = P(('dp', 'ep'), None)
    expert_spec = P('ep', None, None)

    def local_fn(hidden, norm_gain, w_gate, w1_shared, w3_shared, w2_shared, w1_experts, w3_experts, w2_experts, topk_ids):
        def routed_round(base):
            return moe_call(base, norm_gain, w_gate.T, topk_ids.T, hidden, w1_shared, w3_shared, w2_shared,
                            w1_experts, w3_experts, w2_experts)

        out, load = routed_round(None)

        def overflow(state):
            def add_round(i, acc):
                return acc + routed_round(jnp.full((8, 128), i * CAP, F32))[0]

            rounds = jnp.ceil(state[0] / CAP).astype(jnp.int32)
            acc = lax.fori_loop(0, rounds, add_round, jnp.zeros(hidden.shape, F32))
            return jnp.float32(0), acc.astype(BF16)

        return lax.while_loop(lambda state: state[0] > CAP, overflow, (load[0, 0], out))[1]

    return jax.shard_map(local_fn, mesh=mesh, in_specs=(tok_spec, P(), P(), P(), P(), P(), expert_spec, expert_spec, expert_spec, tok_spec), out_specs=tok_spec, check_vma=False)
```

time: 97.9 us -> 77.6 us (0.79)
  Pallas kernels: 91.8 us -> 74.8 us
  other arithmetic: 1.92 us -> 0 us
  local copies, waits for them, and re-layouts: 3.08 us -> 1.77 us
    pallas_call x1, Pallas kernels: 91.8 us -> 74.8 us  [moe_call(): pl.pallas_call(functools.partial(moe_kernel, first), out_shape=(jax.Shape...]
    convert_element_type x1 -> x0, other arithmetic: 1.92 us -> none  [local_fn(): return total.astype(BF16)]
    broadcast_in_dim x2 -> x0, local copies, waits for them, and re-layouts: 1.88 us -> none  [the longest x1 1.29 us: routed_round(): norm_gain[None, :]]
    unnamed x4 -> x5, local copies, waits for them, and re-layouts: 0.01 us -> 1.77 us
    slice x1 -> x0, local copies, waits for them, and re-layouts: 1.19 us -> none  [more(): return state[0] < load[0, 0]]
where the time goes in v2:
time: 77.6 us; the launch traced here: 77.5 us
  Pallas kernels  74.8 us (96%)
  local copies, waits for them, and re-layouts  1.77 us (2%)
  loops' own time  0.82 us (1%)
    pallas_call x1, Pallas kernels, moe_call(): pl.pallas_call(functools.partial(moe_kernel, first), out_shape=(jax.Shape...  74.8 us
    unnamed x5, local copies, waits for them, and re-layouts  1.77 us

profile of v2, /device:TPU:0, one launch (start us, length us, event | category | flops | bytes accessed | tf_op | source)
XLA Modules:
  0.0 77.5 jit_solution(17949073620815052362)
XLA Ops:
  0.0 0.0 copy-start
  0.0 0.0 copy-start.1
  0.0 74.8 %shard_map.100 = (bf16[96,2048]{1,0:T(8,128)(2,1)}, f32[1,1]{1,0:T(1,128)}) custom-call(bf16[2048]{0:T(1024)(128)(2,1)} %refs_0_.1, bf16[64,2048]{1,0:T(8,128)(2,1)} %bitcast.9, s32[6,96]{1,0:T(8,128)} %bitcast.11, bf16[96,2048]{1,0:T(8,128)(2,1)} %refs_3_.1, bf16[2048,2816]{1,0:T(8,128)(2,1)} %refs_4_.1, bf16[2048,2816]{1,0:T(8,128)(2,1)} %refs_5_.1, ...), custom_call_target="tpu_custom_call" | custom-call | tf_op jit(solution)/shard_map/pallas_call | solution.py:360
  74.8 0.0 copy-done
  74.9 0.0 copy-done.1
  74.9 0.8 %while.18 = (f32[]{:T(128)}, bf16[96,2048]{1,0:T(8,128)(2,1)}, bf16[2048,64]{0,1:T(8,128)(2,1)}, s32[96,6]{0,1:T(8,128)S(1)}, bf16[2048]{0:T(1024)(128)(2,1)S(1)...) while((f32[]{:T(128)}, bf16[96,2048]{1,0:T(8,128)(2,1)}, ...), condition=%region_3.0_spmd, body=%region_0.0_spmd | while | flops 393224 | bytes 4329934 | solution.py:421
  75.7 1.8 %copy.28 = bf16[96,2048]{1,0:T(8,128)(2,1)} copy(bf16[96,2048]{1,0:T(8,128)(2,1)} %get-tuple-element.388) | data formatting | bytes 786432
Async XLA Ops:
  0.0 74.8 %copy-start = (bf16[2048]{0:T(1024)(128)(2,1)S(1)}, bf16[2048]{0:T(1024)(128)(2,1)}, u32[]{:S(2)}) copy-start(bf16[2048]{0:T(1024)(128)(2,1)} %refs_0_.1) | copy-start | bytes 12292
  0.0 74.9 %copy-start.1 = (s32[96,6]{0,1:T(8,128)S(1)}, s32[96,6]{0,1:T(8,128)}, u32[]{:S(2)}) copy-start(s32[96,6]{0,1:T(8,128)} %param.23) | copy-start | bytes 6916

commit v3 on v2

--- a/solution.py
+++ b/solution.py
@@ -209,14 +209,17 @@
     slot_row = lax.broadcasted_iota(jnp.int32, (CAP, tokens), 0).astype(F32)
     width = ball.shape[2]
 
+    def gather(e):
+        pick = jnp.where(rk_ref[pl.ds(e, 1), :] == slot_row, 1.0, 0.0).astype(BF16)
+        for k in range(0, width, WIDE):
+            xg_ref[e % 2, :, k:k + WIDE] = dot_f32(pick, ball[:, :, k:k + WIDE].reshape(tokens, WIDE)).astype(BF16)
+
     def stage_one(e, carry):
         s = (e + 2) % RING
-        pick = jnp.where(rk_ref[pl.ds(e, 1), :] == slot_row, 1.0, 0.0).astype(BF16)
-        for k in range(0, width, WIDE):
-            xg_ref[:, k:k + WIDE] = dot_f32(pick, ball[:, :, k:k + WIDE].reshape(tokens, WIDE)).astype(BF16)
         wait_full(s, 0)
         wait_full(s, 1)
-        up_project(xg_ref, s, act_ref.at[e], 0)
+        up_project(xg_ref.at[e % 2], s, act_ref.at[e], 0)
+        gather(e + 1)
 
         @pl.when(e + RING < experts)
         def _():
@@ -228,6 +231,7 @@
 
         return carry
 
+    gather(0)
     lax.fori_loop(0, experts, stage_one, 0)
 
     for cp in (x_v, y_v, d_v, p_v, x_h0, y_h1, x_h1, y_h0, p_own, p_xv, p_yv, p_dv, f_h0, f_h1, p_x, p_y, p_d0, p_d1):
@@ -237,24 +241,25 @@
 
     def send_d(c):
         return pltpu.make_async_remote_copy(
-            src_ref=obuf.at[c % 2], dst_ref=dbuf.at[c % 2], send_sem=ds_sem.at[c], recv_sem=dr_sem.at[c],
+            src_ref=obuf.at[c % 2], dst_ref=dbuf.at[c % 2], send_sem=ds_sem.at[c % 2], recv_sem=dr_sem.at[c % 2],
             device_id={"ep": partner}, device_id_type=pl.DeviceIdType.MESH)
 
     def send_a(c, i):
         return pltpu.make_async_remote_copy(
             src_ref=pbuf.at[c, dq, pl.ds(i * half, half)], dst_ref=abuf.at[c, i],
-            send_sem=as_sem.at[c, i], recv_sem=ar_sem.at[c, i],
+            send_sem=as_sem.at[c % 4, i], recv_sem=ar_sem.at[c % 4, i],
             device_id={"ep": (xdev, ydev)[i]}, device_id_type=pl.DeviceIdType.MESH)
 
-    def send_b(c, i, h):
+    def send_b(c, i, h=None):
+        own = pl.ds(0, rows) if h is None else pl.ds(h * half, half)
         return pltpu.make_async_remote_copy(
-            src_ref=pbuf.at[c, (xq, yq)[i], pl.ds(h * half, half)], dst_ref=rbuf.at[c, i, h],
-            send_sem=bs_sem.at[c, i, h], recv_sem=br_sem.at[c, i, h],
+            src_ref=pbuf.at[c, (xq, yq)[i], own], dst_ref=rbuf.at[c, i, own],
+            send_sem=bs_sem.at[c % 4, i], recv_sem=br_sem.at[c, i],
             device_id={"ep": (xdev, ydev)[i]}, device_id_type=pl.DeviceIdType.MESH)
 
     def out_copy(c):
         cols = pl.ds(pl.multiple_of(c * CHUNK, CHUNK), CHUNK)
-        return pltpu.make_async_copy(out_ref.at[:, cols], out_hbm.at[:, cols], out_sem.at[c])
+        return pltpu.make_async_copy(out_ref.at[:, cols], out_hbm.at[:, cols], out_sem.at[c % 2])
 
     def down_project(c):
         s = (c + experts + 2) % RING
@@ -312,13 +317,16 @@
         local = y_ref[:, cols].astype(F32) + s_ref[:, cols].astype(F32)
         if not first:
             local = jnp.where(base == 0.0, local, 0.0)
-        for h in range(2):
-            part = slice(h * half, (h + 1) * half)
-            routed = pbuf[c, chip, part]
-            for i in range(2):
-                send_b(c, i, h).wait_recv()
-                routed = routed + rbuf[c, i, h]
-            out_ref[part, cols] = (local[part] + routed).astype(out_ref.dtype)
+        routed = pbuf[c, chip]
+        for i in range(2):
+            send_b(c, i).wait_recv()
+            routed = routed + rbuf[c, i]
+
+        @pl.when(c >= 2)
+        def _():
+            out_copy(c - 2).wait()
+
+        out_ref[:, cols] = (local + routed).astype(out_ref.dtype)
         out_copy(c).start()
 
         @pl.when(c >= chunks - 2)
@@ -327,8 +335,7 @@
 
         for i in range(2):
             send_a(c, i).wait_send()
-            for h in range(2):
-                send_b(c, i, h).wait_send()
+            send_b(c, i).wait_send()
 
     def stage_two(c, carry):
         pl.when(c < chunks)(lambda: down_project(c))
@@ -344,7 +351,7 @@
         out_copy(c).wait()
         return carry
 
-    lax.fori_loop(0, chunks, drain, 0)
+    lax.fori_loop(chunks - 2, chunks, drain, 0)
 
 
 def moe_call(base, gain, wgt, idst, y, w1s, w3s, w2s, w1e, w3e, w2e):
@@ -372,27 +379,27 @@
             pltpu.VMEM((2 * experts, tokens), F32),
             pltpu.VMEM((tokens, 128), F32),
             pltpu.VMEM((experts, tokens, CAP), BF16),
-            pltpu.VMEM((CAP, width), BF16),
+            pltpu.VMEM((2, CAP, width), BF16),
             pltpu.VMEM((experts, CAP, ff), BF16),
             pltpu.VMEM((rows, 2 * ff), BF16),
             pltpu.VMEM((chunks, 4, rows, CHUNK), F32),
             pltpu.VMEM((2, 4, rows, CHUNK), F32),
             pltpu.VMEM((2, 4, rows, CHUNK), F32),
             pltpu.VMEM((chunks, 2, rows // 2, CHUNK), F32),
-            pltpu.VMEM((chunks, 2, 2, rows // 2, CHUNK), F32),
+            pltpu.VMEM((chunks, 2, rows, CHUNK), F32),
             pltpu.VMEM((rows, width), BF16),
             pltpu.VMEM((experts, CAP, CHUNK), BF16),
-            dma((chunks,)),
+            dma((2,)),
             dma,
             dma((RING, 2)),
             dma((18,)),
             dma((18,)),
-            dma((chunks,)),
-            dma((chunks,)),
+            dma((2,)),
+            dma((2,)),
+            dma((4, 2)),
+            dma((4, 2)),
+            dma((4, 2)),
             dma((chunks, 2)),
-            dma((chunks, 2)),
-            dma((chunks, 2, 2)),
-            dma((chunks, 2, 2)),
         ],
         compiler_params=pltpu.CompilerParams(
             collective_id=0 if first else 1, has_side_effects=True, vmem_limit_bytes=67_000_000),
@@ -410,14 +417,14 @@
 
         out, load = routed_round(None)
 
-        def overflow(state):
+        def overflow(load, out):
             def add_round(i, acc):
                 return acc + routed_round(jnp.full((8, 128), i * CAP, F32))[0]
 
-            rounds = jnp.ceil(state[0] / CAP).astype(jnp.int32)
+            rounds = jnp.ceil(load / CAP).astype(jnp.int32)
             acc = lax.fori_loop(0, rounds, add_round, jnp.zeros(hidden.shape, F32))
-            return jnp.float32(0), acc.astype(BF16)
-
-        return lax.while_loop(lambda state: state[0] > CAP, overflow, (load[0, 0], out))[1]
+            return acc.astype(BF16)
+
+        return lax.cond(load[0, 0] > CAP, overflow, lambda load, out: out, load[0, 0], out)
 
     return jax.shard_map(local_fn, mesh=mesh, in_specs=(tok_spec, P(), P(), P(), P(), P(), expert_spec, expert_spec, expert_spec, tok_spec), out_specs=tok_spec, check_vma=False)

time: 77.6 us -> 76.2 us (0.982)
  Pallas kernels: 74.8 us -> 73.4 us
    pallas_call x1, Pallas kernels: 74.8 us -> 73.4 us  [moe_call(): pl.pallas_call(functools.partial(moe_kernel, first), out_shape=(jax.Shape...]
    unnamed x5 -> x1, local copies, waits for them, and re-layouts: 1.77 us -> 1.77 us
where the time goes in v3:
time: 76.2 us; the launch traced here: 76 us
  Pallas kernels  73.4 us (96%)
  local copies, waits for them, and re-layouts  1.77 us (2%)
    pallas_call x1, Pallas kernels, moe_call(): pl.pallas_call(functools.partial(moe_kernel, first), out_shape=(jax.Shape...  73.4 us
    unnamed x1, local copies, waits for them, and re-layouts  1.77 us

profile of v3, /device:TPU:0, one launch (start us, length us, event | category | flops | bytes accessed | tf_op | source)
XLA Modules:
  0.0 76.0 jit_solution(8178853099071528094)
XLA Ops:
  0.0 73.4 %shard_map.102 = (bf16[96,2048]{1,0:T(8,128)(2,1)}, f32[1,1]{1,0:T(1,128)}) custom-call(bf16[2048]{0:T(1024)(128)(2,1)} %refs_0_.1, bf16[64,2048]{1,0:T(8,128)(2,1)} %bitcast.9, s32[6,96]{1,0:T(8,128)} %bitcast.11, bf16[96,2048]{1,0:T(8,128)(2,1)} %refs_3_.1, bf16[2048,2816]{1,0:T(8,128)(2,1)} %refs_4_.1, bf16[2048,2816]{1,0:T(8,128)(2,1)} %refs_5_.1, ...), custom_call_target="tpu_custom_call" | custom-call | tf_op jit(solution)/shard_map/pallas_call | solution.py:367
  74.0 0.2 conditional.1
  74.2 1.8 %copy.24 = bf16[96,2048]{1,0:T(8,128)(2,1)} copy(bf16[96,2048]{1,0:T(8,128)(2,1)} %get-tuple-element.115) | data formatting | bytes 786432

commit v4 on v3

--- a/solution.py
+++ b/solution.py
@@ -232,7 +232,12 @@
         return carry
 
     gather(0)
-    lax.fori_loop(0, experts, stage_one, 0)
+    last = experts - 1
+    lax.fori_loop(0, last, stage_one, 0)
+    wait_full((last + 2) % RING, 0)
+    wait_full((last + 2) % RING, 1)
+    up_project(xg_ref.at[last % 2], (last + 2) % RING, act_ref.at[last], 0)
+    issue_down(RING - 1, (last + 2) % RING)
 
     for cp in (x_v, y_v, d_v, p_v, x_h0, y_h1, x_h1, y_h0, p_own, p_xv, p_yv, p_dv, f_h0, f_h1, p_x, p_y, p_d0, p_d1):
         cp.wait_send()

time: 76.2 us -> 76 us (level)
  no operation moved by 1% of the time
where the time goes in v4:
time: 76 us; the launch traced here: 75.9 us
  Pallas kernels  73.3 us (96%)
  local copies, waits for them, and re-layouts  1.77 us (2%)
    pallas_call x1, Pallas kernels, moe_call(): pl.pallas_call(functools.partial(moe_kernel, first), out_shape=(jax.Shape...  73.3 us
    unnamed x1, local copies, waits for them, and re-layouts  1.77 us

profile of v4, /device:TPU:0, one launch (start us, length us, event | category | flops | bytes accessed | tf_op | source)
XLA Modules:
  0.0 75.9 jit_solution(2230116254440552448)
XLA Ops:
  0.0 73.3 %shard_map.102 = (bf16[96,2048]{1,0:T(8,128)(2,1)}, f32[1,1]{1,0:T(1,128)}) custom-call(bf16[2048]{0:T(1024)(128)(2,1)} %refs_0_.1, bf16[64,2048]{1,0:T(8,128)(2,1)} %bitcast.9, s32[6,96]{1,0:T(8,128)} %bitcast.11, bf16[96,2048]{1,0:T(8,128)(2,1)} %refs_3_.1, bf16[2048,2816]{1,0:T(8,128)(2,1)} %refs_4_.1, bf16[2048,2816]{1,0:T(8,128)(2,1)} %refs_5_.1, ...), custom_call_target="tpu_custom_call" | custom-call | tf_op jit(solution)/shard_map/pallas_call | solution.py:372
  73.9 0.2 conditional.1
  74.1 1.8 %copy.24 = bf16[96,2048]{1,0:T(8,128)(2,1)} copy(bf16[96,2048]{1,0:T(8,128)(2,1)} %get-tuple-element.115) | data formatting | bytes 786432

commit v5 on v4

--- a/solution.py
+++ b/solution.py
@@ -91,8 +91,6 @@
         pl.semaphore_signal(barrier, inc=1, device_id={"ep": dev}, device_id_type=pl.DeviceIdType.MESH)
     issue_shared(0, 0)
     issue_shared(1, 1)
-    issue_expert(0, 2)
-    issue_expert(1, 3)
 
     rows_f = y_ref[...].astype(F32)
     inv_rms = lax.rsqrt(jnp.mean(rows_f * rows_f, axis=-1, keepdims=True) + NORM_EPS)
@@ -140,6 +138,8 @@
 
     wait_full(0, 0)
     wait_full(0, 1)
+    issue_expert(0, 2)
+    issue_expert(1, 3)
     up_project(ball.at[me], 0, act_s, 0)
     issue_expert(2, 0)
     x_v.wait_recv()

time: 76 us -> 76 us (level)
  no operation moved by 1% of the time
where the time goes in v5:
time: 76 us; the launch traced here: 75.9 us
  Pallas kernels  73.3 us (96%)
  local copies, waits for them, and re-layouts  1.77 us (2%)
    pallas_call x1, Pallas kernels, moe_call(): pl.pallas_call(functools.partial(moe_kernel, first), out_shape=(jax.Shape...  73.3 us
    unnamed x1, local copies, waits for them, and re-layouts  1.77 us

profile of v5, /device:TPU:0, one launch (start us, length us, event | category | flops | bytes accessed | tf_op | source)
XLA Modules:
  0.0 75.9 jit_solution(13787292618673373478)
XLA Ops:
  0.0 73.3 %shard_map.102 = (bf16[96,2048]{1,0:T(8,128)(2,1)}, f32[1,1]{1,0:T(1,128)}) custom-call(bf16[2048]{0:T(1024)(128)(2,1)} %refs_0_.1, bf16[64,2048]{1,0:T(8,128)(2,1)} %bitcast.9, s32[6,96]{1,0:T(8,128)} %bitcast.11, bf16[96,2048]{1,0:T(8,128)(2,1)} %refs_3_.1, bf16[2048,2816]{1,0:T(8,128)(2,1)} %refs_4_.1, bf16[2048,2816]{1,0:T(8,128)(2,1)} %refs_5_.1, ...), custom_call_target="tpu_custom_call" | custom-call | tf_op jit(solution)/shard_map/pallas_call | solution.py:372
  73.9 0.2 conditional.1
  74.1 1.8 %copy.24 = bf16[96,2048]{1,0:T(8,128)(2,1)} copy(bf16[96,2048]{1,0:T(8,128)(2,1)} %get-tuple-element.115) | data formatting | bytes 786432
